TPU v7x, 32 devices: a whole 2x2x4 slice. The times are simulated.
32 devices in a mesh: bx: 4 (over z), by: 2 (over x), bz: 4 (over y, core).
Axes of the slice: x: 2, y: 2, z: 4, core: 2. Of those that a mesh axis runs over, the one named last changes fastest.
Arguments:
- estimate: float32 [64, 32, 512], P('bx', 'by', 'bz'), may hold values from 0.2 to 5
- observed: float32 [8, 64, 32, 512], P(None, 'bx', 'by', 'bz'), may hold values from 0.3 to 180, as said below
- coverage: int32 [8, 4, 2, 4], P(None, 'bx', 'by', 'bz'), may hold values from 0 to 1, as said below
- psf_taps: float32 [8, 3, 17], replicated, may hold values from 0.05 to 1
Outputs:
- refined: float32 [64, 32, 512], P('bx', 'by', 'bz')
Inputs may be any that keep to these rules, and one draw needn't show every extreme that they name: `coverage`: each block is covered by 2 to 8 views; in every draw some block is covered by all 8. `observed`: positive.
All inputs are finite; a program needn't handle non-finite values.
Results may differ from a plain program's by a relative error of at most 0.0001.
Values sent between devices are 32-bit elements; how exact they have to be, the bound alone decides.
A program may use at most 64 MiB of HBM per device.

v0:
```python
import functools

import jax
import jax.numpy as jnp
from jax import lax
from jax.experimental import pallas as pl
from jax.experimental.pallas import tpu as pltpu
from jax.sharding import PartitionSpec as P

F32 = jnp.float32
BF16 = jnp.bfloat16
MESH = pl.DeviceIdType.MESH


def split(values):
    high = values.astype(BF16)
    low = (values - high.astype(F32)).astype(BF16)
    return high, low


def dot3(left, right, dims=((1,), (0,))):
    def one(a, b):
        return lax.dot_general(a, b, (dims, ((), ())), preferred_element_type=F32)

    return one(left[0], right[0]) + (one(left[0], right[1]) + one(left[1], right[0]))


def kernel(
    sizes,
    taps_ref,
    cover_ref,
    est_ref,
    obs_hbm,
    out_ref,
    obs,
    ext,
    ext_hi,
    ext_lo,
    pack,
    from_left,
    from_right,
    weight,
    weight_xy,
    weight_left,
    weight_right,
    scale,
    band_hi,
    band_lo,
    gath_hi,
    gath_lo,
    scat_hi,
    scat_lo,
    lined,
    spread,
    total,
    fringe,
    back_pack,
    back_left,
    back_right,
    back_xy,
    stat,
    stat_a,
    stat_b,
    part_a,
    obs_sem,
    xy_send,
    xy_recv,
    wxy_send,
    wxy_recv,
    z_send,
    z_recv,
    bz_send,
    bz_recv,
    bxy_send,
    bxy_recv,
    a_send,
    a_recv,
    b_send,
    b_recv,
):
    n_x, n_y, n_z = sizes
    views, rows, cols, lanes = obs.shape
    length = taps_ref.shape[2]
    rad = (length - 1) // 2
    wide_x, wide_y = rows + 2 * rad, cols + 2 * rad
    groups = wide_x // 8
    me_x, me_y, me_z = lax.axis_index("bx"), lax.axis_index("by"), lax.axis_index("bz")

    fetch = pltpu.make_async_copy(obs_hbm, obs, obs_sem)
    fetch.start()

    def exists(dx, dy, dz):
        ok = None
        for step, me, count in ((dx, me_x, n_x), (dy, me_y, n_y), (dz, me_z, n_z)):
            if step == 0:
                continue
            inside = (me + step >= 0) & (me + step < count)
            ok = inside if ok is None else ok & inside
        return ok

    def device(dx, dy, dz):
        return {"bx": me_x + dx, "by": me_y + dy, "bz": me_z + dz}

    around = [(dx, dy) for dx in (-1, 0, 1) for dy in (-1, 0, 1) if (dx, dy) != (0, 0)]
    ring_a = [(i, j) for i in range(n_y) for j in range(n_z) if (i, j) != (0, 0)]

    def device_a(i, j):
        return {"bx": me_x, "by": lax.rem(me_y + i, n_y), "bz": lax.rem(me_z + j, n_z)}

    def device_b(i):
        return {"bx": lax.rem(me_x + i, n_x), "by": me_y, "bz": me_z}

    ext[...] = jnp.zeros(ext.shape, F32)
    ext[rad : rad + rows, rad : rad + cols, :] = est_ref[...]
    from_left[...] = jnp.zeros(from_left.shape, F32)
    from_right[...] = jnp.zeros(from_right.shape, F32)
    weight_xy[...] = jnp.zeros(weight_xy.shape, F32)
    weight_left[...] = jnp.zeros(weight_left.shape, F32)
    weight_right[...] = jnp.zeros(weight_right.shape, F32)
    back_xy[...] = jnp.zeros(back_xy.shape, F32)
    back_left[...] = jnp.zeros(back_left.shape, F32)
    back_right[...] = jnp.zeros(back_right.shape, F32)
    for v in range(views):
        row = jnp.full((1, lanes), cover_ref[v], jnp.int32).astype(F32)
        weight[v : v + 1, :] = row
        weight_xy[1, 1, v : v + 1, :] = row

    barrier = pltpu.get_barrier_semaphore()
    expected = len(ring_a) + n_x - 1
    for i, j in ring_a:
        pl.semaphore_signal(barrier, inc=1, device_id=device_a(i, j), device_id_type=MESH)
    for i in range(1, n_x):
        pl.semaphore_signal(barrier, inc=1, device_id=device_b(i), device_id_type=MESH)
    for dx, dy in around:
        if dx != 0 and dy != 0:
            ok = exists(dx, dy, 0)

            @pl.when(ok)
            def _():
                pl.semaphore_signal(barrier, inc=1, device_id=device(dx, dy, 0), device_id_type=MESH)

            expected = expected + ok.astype(jnp.int32)
    pl.semaphore_wait(barrier, expected)

    def cut(step, size):
        return pl.ds(0, size) if step == 0 else (pl.ds(0, rad) if step < 0 else pl.ds(size - rad, rad))

    def wide(step, size):
        return pl.ds(rad, size) if step == 0 else (pl.ds(0, rad) if step < 0 else pl.ds(rad + size, rad))

    def xy_copies():
        for slot, (dx, dy) in enumerate(around):
            copies = [
                pltpu.make_async_remote_copy(
                    src_ref=est_ref.at[cut(dx, rows), cut(dy, cols), :],
                    dst_ref=ext.at[wide(-dx, rows), wide(-dy, cols), :],
                    send_sem=xy_send.at[slot],
                    recv_sem=xy_recv.at[slot],
                    device_id=device(dx, dy, 0),
                    device_id_type=MESH,
                ),
                pltpu.make_async_remote_copy(
                    src_ref=weight,
                    dst_ref=weight_xy.at[1 - dx, 1 - dy],
                    send_sem=wxy_send.at[slot],
                    recv_sem=wxy_recv.at[slot],
                    device_id=device(dx, dy, 0),
                    device_id_type=MESH,
                ),
            ]
            yield exists(dx, dy, 0), exists(-dx, -dy, 0), copies

    def z_copies():
        for slot, (dz, pack_to, weight_to) in enumerate(
            ((-1, from_right, weight_right), (1, from_left, weight_left))
        ):
            copies = [
                pltpu.make_async_remote_copy(
                    src_ref=source,
                    dst_ref=target,
                    send_sem=z_send.at[slot, which],
                    recv_sem=z_recv.at[slot, which],
                    device_id=device(0, 0, dz),
                    device_id_type=MESH,
                )
                for which, (source, target) in enumerate(((pack, pack_to), (weight_xy, weight_to)))
            ]
            yield exists(0, 0, dz), exists(0, 0, -dz), copies

    def back_z_copies():
        for slot, (dz, target) in enumerate(((-1, back_right), (1, back_left))):
            copy = pltpu.make_async_remote_copy(
                src_ref=back_pack,
                dst_ref=target,
                send_sem=bz_send.at[slot],
                recv_sem=bz_recv.at[slot],
                device_id=device(0, 0, dz),
                device_id_type=MESH,
            )
            yield exists(0, 0, dz), exists(0, 0, -dz), [copy]

    def back_xy_copies():
        for slot, (dx, dy) in enumerate(around):
            copy = pltpu.make_async_remote_copy(
                src_ref=total.at[wide(dx, rows), wide(dy, cols), :],
                dst_ref=back_xy.at[wide(-dx, rows), wide(-dy, cols), :],
                send_sem=bxy_send.at[slot],
                recv_sem=bxy_recv.at[slot],
                device_id=device(dx, dy, 0),
                device_id_type=MESH,
            )
            yield exists(dx, dy, 0), exists(-dx, -dy, 0), [copy]

    def start(family):
        for sends, _, copies in family():

            @pl.when(sends)
            def _():
                for copy in copies:
                    copy.start()

    def arrive(family):
        for _, takes, copies in family():

            @pl.when(takes)
            def _():
                for copy in copies:
                    copy.wait_recv()

    def leave(family):
        for sends, _, copies in family():

            @pl.when(sends)
            def _():
                for copy in copies:
                    copy.wait_send()

    start(xy_copies)

    def build(v, carry):
        def summed(dim):
            values = [taps_ref[v, dim, k] for k in range(length)]
            while len(values) > 1:
                values = [sum(values[i : i + 2]) for i in range(0, len(values), 2)]
            return jnp.full((8, lanes), values[0], F32)

        inverse = 1.0 / (summed(0) * summed(1) * summed(2))

        def chosen(offset, dim):
            result = jnp.zeros(offset.shape, F32)
            for k in range(length):
                result = jnp.where(offset == k, taps_ref[v, dim, k], result)
            return result

        def iota(shape, dim):
            return lax.broadcasted_iota(jnp.int32, shape, dim)

        shape = (lanes, lanes)
        main = chosen(iota(shape, 0) - iota(shape, 1) + rad, 2)
        shape = (2 * rad, lanes)
        row, col = iota(shape, 0), iota(shape, 1)
        edge = chosen(jnp.where(row < rad, row, row + lanes) - col, 2)
        for first, part in ((0, main), (lanes, edge)):
            part = (part.reshape(-1, 8, lanes) * inverse[None]).reshape(part.shape)
            high, low = split(part)
            band_hi[v, first : first + part.shape[0], :] = high
            band_lo[v, first : first + part.shape[0], :] = low
        rest = band_hi.shape[1] - lanes - 2 * rad
        band_hi[v, lanes + 2 * rad :, :] = jnp.zeros((rest, lanes), BF16)
        band_lo[v, lanes + 2 * rad :, :] = jnp.zeros((rest, lanes), BF16)
        shape = (8 * cols, 8 * wide_y)
        row, col = iota(shape, 0), iota(shape, 1)
        offset = jnp.where(row // cols == col // wide_y, col % wide_y - row % cols, -1)
        high, low = split(chosen(offset, 1))
        gath_hi[v], gath_lo[v] = high, low
        shape = (8 * wide_y, 8 * cols)
        row, col = iota(shape, 0), iota(shape, 1)
        offset = jnp.where(row // wide_y == col // cols, row % wide_y - col % cols, -1)
        high, low = split(chosen(offset, 1))
        scat_hi[v], scat_lo[v] = high, low
        return carry

    lax.fori_loop(0, views, build, 0)

    fetch.wait()
    count = jnp.zeros((1, lanes), F32)
    seen = jnp.zeros((8, lanes), F32)
    for v in range(views):
        count = count + weight[v : v + 1, :]
        seen = seen + weight[v : v + 1, :] * jnp.sum(obs[v].reshape(-1, 8, lanes), axis=0)
    stat[0] = seen / count

    arrive(xy_copies)
    lane = lax.broadcasted_iota(jnp.int32, (wide_y, lanes), 1)
    for g in range(groups):
        merged = jnp.zeros((wide_y, lanes), F32)
        for i in range(8):
            rolled = pltpu.roll(ext[8 * g + i], 2 * rad * i + rad, 1)
            merged = jnp.where(lane // (2 * rad) == i, rolled, merged)
        pack[g] = merged
    start(z_copies)
    high, low = split(ext[...].reshape(wide_x * wide_y, lanes))
    ext_hi[:, :lanes] = high
    ext_lo[:, :lanes] = low
    arrive(z_copies)
    for g in range(groups):
        merged = jnp.where(lane % (2 * rad) < rad, from_left[g], from_right[g])
        for i in range(8):
            shift = (lanes - 2 * rad * i) % lanes
            rolled = pltpu.roll(merged, shift, 1) if shift else merged
            high, low = split(rolled)
            first = (8 * g + i) * wide_y
            ext_hi[first : first + wide_y, lanes:] = high
            ext_lo[first : first + wide_y, lanes:] = low

    thin = lax.broadcasted_iota(jnp.int32, (rad, lanes), 1)
    for v in range(views):
        for dx in range(3):
            for dy in range(3):
                mid = jnp.broadcast_to(weight_xy[dx, dy, v : v + 1, :], (rad, lanes))
                left = jnp.broadcast_to(weight_left[dx, dy, v : v + 1, :], (rad, lanes))
                right = jnp.broadcast_to(weight_right[dx, dy, v : v + 1, :], (rad, lanes))
                side = jnp.where(thin < rad, left, jnp.where(thin < 2 * rad, right, 0.0))
                for first in range(0 if dy == 0 else (rad if dy == 1 else rad + cols), rad if dy == 0 else (rad + cols if dy == 1 else wide_y), rad):
                    scale[v, dx, first : first + rad, :lanes] = mid
                    scale[v, dx, first : first + rad, lanes:] = side

    total[...] = jnp.zeros(total.shape, F32)
    fringe[...] = jnp.zeros(fringe.shape, F32)

    def one_view(v, carry):
        band = band_hi[v], band_lo[v]
        gath = gath_hi[v], gath_lo[v]
        scat = scat_hi[v], scat_lo[v]
        size = 8 * wide_y
        for g in range(groups):
            here = slice(g * size, (g + 1) * size)
            blurred = dot3((ext_hi[here, :], ext_lo[here, :]), band)
            lined[8 * g : 8 * g + 8] = dot3(gath, split(blurred)).reshape(8, cols, lanes)
        blur = taps_ref[v, 0, 0] * lined[0:rows]
        for k in range(1, length):
            blur = blur + taps_ref[v, 0, k] * lined[k : k + rows]
        spread[...] = obs[v] / blur
        for g in range(groups):
            pieces = []
            for e in range(8 * g, 8 * g + 8):
                piece = None
                for a in range(rows):
                    if 0 <= e - a < length:
                        term = taps_ref[v, 0, e - a] * spread[a]
                        piece = term if piece is None else piece + term
                pieces.append(piece)
            piece = jnp.concatenate(pieces, axis=0)
            piece = dot3(scat, split(piece))
            piece = dot3(split(piece), band, ((1,), (1,))).reshape(8, wide_y, 2 * lanes)
            dx = 0 if 8 * g < rad else (1 if 8 * g < rad + rows else 2)
            piece = piece * scale[v, dx][None]
            total[8 * g : 8 * g + 8] += piece[:, :, :lanes]
            fringe[8 * g : 8 * g + 8] += piece[:, :, lanes:]
        return carry

    lax.fori_loop(0, views, one_view, 0)

    for g in range(groups):
        merged = fringe[8 * g]
        for i in range(1, 8):
            merged = merged + pltpu.roll(fringe[8 * g + i], 2 * rad * i, 1)
        back_pack[g] = merged
    start(back_z_copies)
    arrive(back_z_copies)
    for g in range(groups):
        merged = jnp.where(lane % (2 * rad) < rad, back_right[g], back_left[g])
        for i in range(8):
            rolled = pltpu.roll(merged, lanes - (2 * rad * i + rad), 1)
            total[8 * g + i] += jnp.where((lane < rad) | (lane >= lanes - rad), rolled, 0.0)
    start(back_xy_copies)
    arrive(back_xy_copies)
    near = back_xy[...]

    def fold(values, size, axis):
        low = lax.slice_in_dim(values, 0, rad, axis=axis)
        mid = lax.slice_in_dim(values, rad, rad + size, axis=axis)
        top = lax.slice_in_dim(values, rad + size, 2 * rad + size, axis=axis)
        if size == 2 * rad:
            return mid + jnp.concatenate([low, top], axis=axis)
        gap_shape = list(low.shape)
        gap_shape[axis] = size - rad
        gap = jnp.zeros(gap_shape, F32)
        return mid + jnp.concatenate([low, gap], axis=axis) + jnp.concatenate([gap, top], axis=axis)

    near = fold(fold(near, rows, 0), cols, 1)
    summed = total[rad : rad + rows, rad : rad + cols, :] + near
    updated = est_ref[...] * (summed / count.reshape(1, 1, lanes))
    out_ref[...] = updated
    stat[1] = jnp.sum(updated.reshape(-1, 8, lanes), axis=0)

    def sums_a():
        for slot, (i, j) in enumerate(ring_a):
            yield pltpu.make_async_remote_copy(
                src_ref=stat,
                dst_ref=stat_a.at[slot],
                send_sem=a_send.at[slot],
                recv_sem=a_recv.at[slot],
                device_id=device_a(i, j),
                device_id_type=MESH,
            )

    def sums_b():
        for i in range(1, n_x):
            yield pltpu.make_async_remote_copy(
                src_ref=part_a,
                dst_ref=stat_b.at[i - 1],
                send_sem=b_send.at[i - 1],
                recv_sem=b_recv.at[i - 1],
                device_id=device_b(i),
                device_id_type=MESH,
            )

    for copy in sums_a():
        copy.start()
    for copy in sums_a():
        copy.wait_recv()
    part_a[...] = stat[...] + jnp.sum(stat_a[...], axis=0)
    for copy in sums_b():
        copy.start()
    for copy in sums_b():
        copy.wait_recv()
    everything = part_a[...] + jnp.sum(stat_b[...], axis=0)
    wanted = jnp.sum(jnp.sum(everything[0], axis=0, keepdims=True), axis=1, keepdims=True)
    gotten = jnp.sum(jnp.sum(everything[1], axis=0, keepdims=True), axis=1, keepdims=True)
    factor = jnp.broadcast_to(wanted, (1, lanes)) / jnp.broadcast_to(gotten, (1, lanes))
    out_ref[...] = out_ref[...] * factor.reshape(1, 1, lanes)

    for family in (xy_copies, z_copies, back_z_copies, back_xy_copies):
        leave(family)
    for copy in sums_a():
        copy.wait_send()
    for copy in sums_b():
        copy.wait_send()


def on_device(sizes, estimate, observed, coverage, psf_taps):
    rows, cols, lanes = estimate.shape
    views = observed.shape[0]
    rad = (psf_taps.shape[2] - 1) // 2
    wide_x, wide_y = rows + 2 * rad, cols + 2 * rad
    groups = wide_x // 8
    n_x, n_y, n_z = sizes
    n_a, n_b = n_y * n_z - 1, n_x - 1

    def vm(*shape, dtype=F32):
        return pltpu.VMEM(shape, dtype)

    def dma(*shape):
        return pltpu.SemaphoreType.DMA(shape)

    scratch = [
        vm(*observed.shape),
        vm(wide_x, wide_y, lanes),
        vm(wide_x * wide_y, 2 * lanes, dtype=BF16),
        vm(wide_x * wide_y, 2 * lanes, dtype=BF16),
        vm(groups, wide_y, lanes),
        vm(groups, wide_y, lanes),
        vm(groups, wide_y, lanes),
        vm(views, lanes),
        vm(3, 3, views, lanes),
        vm(3, 3, views, lanes),
        vm(3, 3, views, lanes),
        vm(views, 3, wide_y, 2 * lanes),
        vm(views, 2 * lanes, lanes, dtype=BF16),
        vm(views, 2 * lanes, lanes, dtype=BF16),
        vm(views, 8 * cols, 8 * wide_y, dtype=BF16),
        vm(views, 8 * cols, 8 * wide_y, dtype=BF16),
        vm(views, 8 * wide_y, 8 * cols, dtype=BF16),
        vm(views, 8 * wide_y, 8 * cols, dtype=BF16),
        vm(wide_x, cols, lanes),
        vm(rows, cols, lanes),
        vm(wide_x, wide_y, lanes),
        vm(wide_x, wide_y, lanes),
        vm(groups, wide_y, lanes),
        vm(groups, wide_y, lanes),
        vm(groups, wide_y, lanes),
        vm(wide_x, wide_y, lanes),
        vm(2, 8, lanes),
        vm(n_a, 2, 8, lanes),
        vm(n_b, 2, 8, lanes),
        vm(2, 8, lanes),
        pltpu.SemaphoreType.DMA,
        dma(8),
        dma(8),
        dma(8),
        dma(8),
        dma(2, 2),
        dma(2, 2),
        dma(2),
        dma(2),
        dma(8),
        dma(8),
        dma(n_a),
        dma(n_a),
        dma(n_b),
        dma(n_b),
    ]
    return pl.pallas_call(
        functools.partial(kernel, sizes),
        out_shape=jax.ShapeDtypeStruct(estimate.shape, F32),
        in_specs=[
            pl.BlockSpec(memory_space=pltpu.SMEM),
            pl.BlockSpec(memory_space=pltpu.SMEM),
            pl.BlockSpec(memory_space=pltpu.VMEM),
            pl.BlockSpec(memory_space=pl.ANY),
        ],
        out_specs=pl.BlockSpec(memory_space=pltpu.VMEM),
        scratch_shapes=scratch,
        compiler_params=pltpu.CompilerParams(collective_id=0, has_side_effects=True),
    )(psf_taps, coverage.reshape(views), estimate, observed)


def solution(mesh):
    sizes = tuple(mesh.shape[axis] for axis in ("bx", "by", "bz"))
    return jax.shard_map(
        functools.partial(on_device, sizes),
        mesh=mesh,
        in_specs=(P("bx", "by", "bz"), P(None, "bx", "by", "bz"), P(None, "bx", "by", "bz"), P()),
        out_specs=P("bx", "by", "bz"),
        check_vma=False,
    )
```

profile of v0, /device:TPU:0, one launch (start us, length us, event | category | flops | bytes accessed | tf_op | source)
XLA Modules:
  0.0 53.0 jit_solution(1586234627674081440)
XLA Ops:
  0.0 1.3 %copy.5.taps_ref = f32[8,3,17]{2,1,0:T(4,128)} copy(f32[8,3,17]{2,0,1:T(8,128)} %param.7) | data formatting | bytes 3264 | tf_op args[3]
  1.3 50.1 %shard_map.46 = f32[16,16,128]{2,1,0:T(8,128)} custom-call(f32[8,3,17]{2,1,0:T(4,128)} %copy.5.taps_ref, s32[8]{0:T(128)} %bitcast.1, f32[16,16,128]{2,1,0:T(8,128)} %est_ref.1, f32[8,16,16,128]{3,2,1,0:T(8,128)} %obs_hbm.1), custom_call_target="tpu_custom_call" | custom-call | tf_op jit(solution)/shard_map/pallas_call | solution.py:504
  51.5 1.6 %copy.7 = f32[16,16,128]{2,1,0:T(8,128)} copy(f32[16,16,128]{2,1,0:T(8,128)} %shard_map.46) | data formatting | bytes 262144
where the time goes:
time: 53.3 us; the launch traced here: 53 us
  Pallas kernels  50.1 us (94%)
  local copies, waits for them, and re-layouts  2.88 us (5%)
    pallas_call x1, Pallas kernels, on_device(): pl.pallas_call(functools.partial(kernel, sizes), out_shape=jax.ShapeDtype...  50.1 us
    unnamed x2, local copies, waits for them, and re-layouts  2.88 us

commit v1 on v0

v1 whole, which is shorter than its diff:
```python
import functools

import jax
import jax.numpy as jnp
from jax import lax
from jax.experimental import pallas as pl
from jax.experimental.pallas import tpu as pltpu
from jax.sharding import PartitionSpec as P

F32 = jnp.float32
BF16 = jnp.bfloat16
MESH = pl.DeviceIdType.MESH


def split(values):
    high = values.astype(BF16)
    low = (values - high.astype(F32)).astype(BF16)
    return high, low


def dot(left, right, dims=((1,), (0,))):
    return lax.dot_general(left, right, (dims, ((), ())), preferred_element_type=F32)


def folded(values):
    half = values.shape[1] // 2
    return values[:, :half] + values[:, half:]


def rings(sizes):
    offsets = [(i, j, k) for i in range(sizes[0]) for j in range(sizes[1]) for k in range(sizes[2])]
    offsets = offsets[1:]
    if len(offsets) < 64:
        return offsets, offsets, []
    return (
        offsets,
        [offset for offset in offsets if offset[0] == 0],
        [offset for offset in offsets if offset[1:] == (0, 0)],
    )


def kernel(
    sizes,
    taps_ref,
    cover_ref,
    est_ref,
    obs_hbm,
    out_ref,
    obs,
    ext,
    ext_hi,
    ext_lo,
    pack,
    from_left,
    from_right,
    weight,
    weight_xy,
    weight_left,
    weight_right,
    scale,
    band,
    twin,
    gath_hi,
    gath_lo,
    scat,
    lined,
    spread,
    total,
    fringe,
    back_pack,
    back_left,
    back_right,
    back_xy,
    stat,
    stat_a,
    stat_b,
    part_a,
    obs_sem,
    out_send,
    out_recv,
    back_send,
    back_recv,
    a_send,
    a_recv,
    b_send,
    b_recv,
):
    n_x, n_y, n_z = sizes
    views, rows, cols, lanes = obs.shape
    length = taps_ref.shape[2]
    rad = (length - 1) // 2
    wide_x, wide_y = rows + 2 * rad, cols + 2 * rad
    groups = wide_x // 8
    me_x, me_y, me_z = lax.axis_index("bx"), lax.axis_index("by"), lax.axis_index("bz")

    fetch = pltpu.make_async_copy(obs_hbm, obs, obs_sem)
    fetch.start()

    def exists(dx, dy, dz):
        ok = None
        for step, me, count in ((dx, me_x, n_x), (dy, me_y, n_y), (dz, me_z, n_z)):
            if step == 0:
                continue
            inside = (me + step >= 0) & (me + step < count)
            ok = inside if ok is None else ok & inside
        return ok

    def device(dx, dy, dz):
        return {"bx": me_x + dx, "by": me_y + dy, "bz": me_z + dz}

    steps = (-1, 0, 1)
    around = [(dx, dy, dz) for dz in steps for dx in steps for dy in steps if (dx, dy, dz) != (0, 0, 0)]
    ring_all, ring_a, ring_b = rings(sizes)

    def partner(i, j, k):
        return {
            "bx": lax.rem(me_x + i, n_x),
            "by": lax.rem(me_y + j, n_y),
            "bz": lax.rem(me_z + k, n_z),
        }

    ext[...] = jnp.zeros(ext.shape, F32)
    ext[rad : rad + rows, rad : rad + cols, :] = est_ref[...]
    from_left[...] = jnp.zeros(from_left.shape, F32)
    from_right[...] = jnp.zeros(from_right.shape, F32)
    weight_xy[...] = jnp.zeros(weight_xy.shape, F32)
    weight_left[...] = jnp.zeros(weight_left.shape, F32)
    weight_right[...] = jnp.zeros(weight_right.shape, F32)
    back_xy[...] = jnp.zeros(back_xy.shape, F32)
    back_left[...] = jnp.zeros(back_left.shape, F32)
    back_right[...] = jnp.zeros(back_right.shape, F32)
    for v in range(views):
        row = jnp.full((1, lanes), cover_ref[v], jnp.int32).astype(F32)
        weight[v : v + 1, :] = row
        weight_xy[1, 1, v : v + 1, :] = row

    barrier = pltpu.get_barrier_semaphore()
    for offset in ring_all:
        pl.semaphore_signal(barrier, inc=1, device_id=partner(*offset), device_id_type=MESH)

    lane = lax.broadcasted_iota(jnp.int32, (cols, lanes), 1)
    for g in range(rows // 8):
        merged = jnp.zeros((cols, lanes), F32)
        for i in range(8):
            rolled = pltpu.roll(est_ref[8 * g + i], 2 * rad * i + rad, 1)
            merged = jnp.where(lane // (2 * rad) == i, rolled, merged)
        pack[g] = merged

    def cut(step, size, width):
        return pl.ds(0, size) if step == 0 else pl.ds(0 if step < 0 else size - width, width)

    def wide(step, size, width):
        return pl.ds(width, size) if step == 0 else pl.ds(0 if step < 0 else width + size, width)

    pack_rows, pack_rad = rows // 8, rad // 8

    def out_copies():
        for slot, (dx, dy, dz) in enumerate(around):
            size, width = (rows, rad) if dz == 0 else (pack_rows, pack_rad)
            source = est_ref if dz == 0 else pack
            target = (from_right, ext, from_left)[dz + 1]
            weights = (weight_right, weight_xy, weight_left)[dz + 1]
            pairs = (
                (
                    source.at[cut(dx, size, width), cut(dy, cols, rad), :],
                    target.at[wide(-dx, size, width), wide(-dy, cols, rad), :],
                ),
                (weight, weights.at[1 - dx, 1 - dy]),
            )
            copies = [
                pltpu.make_async_remote_copy(
                    src_ref=pair[0],
                    dst_ref=pair[1],
                    send_sem=out_send.at[slot, which],
                    recv_sem=out_recv.at[slot, which],
                    device_id=device(dx, dy, dz),
                    device_id_type=MESH,
                )
                for which, pair in enumerate(pairs)
            ]
            yield exists(dx, dy, dz), exists(-dx, -dy, -dz), copies

    def back_copies():
        for slot, (dx, dy, dz) in enumerate(around):
            size, width = (rows, rad) if dz == 0 else (pack_rows, pack_rad)
            source = total if dz == 0 else back_pack
            target = (back_right, back_xy, back_left)[dz + 1]
            copy = pltpu.make_async_remote_copy(
                src_ref=source.at[wide(dx, size, width), wide(dy, cols, rad), :],
                dst_ref=target.at[wide(-dx, size, width), wide(-dy, cols, rad), :],
                send_sem=back_send.at[slot],
                recv_sem=back_recv.at[slot],
                device_id=device(dx, dy, dz),
                device_id_type=MESH,
            )
            yield exists(dx, dy, dz), exists(-dx, -dy, -dz), [copy]

    def start(family):
        for sends, _, copies in family():

            @pl.when(sends)
            def _():
                for copy in copies:
                    copy.start()

    def arrive(family):
        for _, takes, copies in family():

            @pl.when(takes)
            def _():
                for copy in copies:
                    copy.wait_recv()

    def leave(family):
        for sends, _, copies in family():

            @pl.when(sends)
            def _():
                for copy in copies:
                    copy.wait_send()

    def build(v, carry):
        def summed(dim):
            values = [taps_ref[dim, v, k] for k in range(length)]
            while len(values) > 1:
                values = [sum(values[i : i + 2]) for i in range(0, len(values), 2)]
            return jnp.full((8, lanes), values[0], F32)

        inverse = 1.0 / (summed(0) * summed(1) * summed(2))

        def chosen(offset, dim):
            result = jnp.zeros(offset.shape, F32)
            for k in range(length):
                result = jnp.where(offset == k, taps_ref[dim, v, k], result)
            return result

        def iota(shape, dim):
            return lax.broadcasted_iota(jnp.int32, shape, dim)

        shape = (lanes, lanes)
        main = chosen(iota(shape, 0) - iota(shape, 1) + rad, 2)
        shape = (2 * rad, lanes)
        row, col = iota(shape, 0), iota(shape, 1)
        edge = chosen(jnp.where(row < rad, row, row + lanes) - col, 2)
        for first, part in ((0, main), (lanes, edge)):
            part = (part.reshape(-1, 8, lanes) * inverse[None]).reshape(part.shape)
            high, low = split(part)
            band[v, first : first + part.shape[0], :] = jnp.concatenate([high, low], axis=1)
            twin[v, first : first + part.shape[0], :] = jnp.concatenate([high, high], axis=1)
        rest = band.shape[1] - lanes - 2 * rad
        band[v, lanes + 2 * rad :, :] = jnp.zeros((rest, 2 * lanes), BF16)
        twin[v, lanes + 2 * rad :, :] = jnp.zeros((rest, 2 * lanes), BF16)
        shape = (8 * cols, 8 * wide_y)
        row, col = iota(shape, 0), iota(shape, 1)
        offset = jnp.where(row // cols == col // wide_y, col % wide_y - row % cols, -1)
        high, low = split(chosen(offset, 1))
        gath_hi[v], gath_lo[v] = high, low
        shape = (8 * wide_y, 8 * cols)
        row, col = iota(shape, 0), iota(shape, 1)
        offset = jnp.where(row // wide_y == col // cols, row % wide_y - col % cols, -1)
        high, low = split(chosen(offset, 1))
        scat[v] = jnp.concatenate([high, low], axis=1)
        return carry

    early = min(3, views)
    lax.fori_loop(0, early, build, 0)
    pl.semaphore_wait(barrier, len(ring_all))
    start(out_copies)
    lax.fori_loop(early, views, build, 0)

    fetch.wait()
    count = jnp.zeros((1, lanes), F32)
    seen = jnp.zeros((8, lanes), F32)
    for v in range(views):
        count = count + weight[v : v + 1, :]
        seen = seen + weight[v : v + 1, :] * jnp.sum(obs[v].reshape(-1, 8, lanes), axis=0)
    stat[0:1] = jnp.sum(seen / count, axis=0, keepdims=True)

    arrive(out_copies)
    lane = lax.broadcasted_iota(jnp.int32, (wide_y, lanes), 1)
    high, low = split(ext[...].reshape(wide_x * wide_y, lanes))
    ext_hi[:, :lanes] = high
    ext_lo[:, :lanes] = low
    for g in range(groups):
        merged = jnp.where(lane % (2 * rad) < rad, from_left[g], from_right[g])
        for i in range(8):
            shift = (lanes - 2 * rad * i) % lanes
            rolled = pltpu.roll(merged, shift, 1) if shift else merged
            high, low = split(rolled)
            first = (8 * g + i) * wide_y
            ext_hi[first : first + wide_y, lanes:] = high
            ext_lo[first : first + wide_y, lanes:] = low

    thin = lax.broadcasted_iota(jnp.int32, (rad, lanes), 1)
    for v in range(views):
        for dx in range(3):
            for dy in range(3):
                mid = jnp.broadcast_to(weight_xy[dx, dy, v : v + 1, :], (rad, lanes))
                left = jnp.broadcast_to(weight_left[dx, dy, v : v + 1, :], (rad, lanes))
                right = jnp.broadcast_to(weight_right[dx, dy, v : v + 1, :], (rad, lanes))
                side = jnp.where(thin < rad, left, jnp.where(thin < 2 * rad, right, 0.0))
                for first in range(0 if dy == 0 else (rad if dy == 1 else rad + cols), rad if dy == 0 else (rad + cols if dy == 1 else wide_y), rad):
                    scale[v, dx, first : first + rad, :lanes] = mid
                    scale[v, dx, first : first + rad, lanes:] = side

    total[...] = jnp.zeros(total.shape, F32)
    fringe[...] = jnp.zeros(fringe.shape, F32)

    def one_view(v, carry):
        size = 8 * wide_y
        high_part = slice(0, lanes)
        for g in range(groups):
            here = slice(g * size, (g + 1) * size)
            blurred = folded(dot(ext_hi[here, :], band[v])) + dot(ext_lo[here, :], band[v, :, high_part])
            high, low = split(blurred)
            line = folded(dot(gath_hi[v], jnp.concatenate([high, low], axis=1))) + dot(gath_lo[v], high)
            lined[8 * g : 8 * g + 8] = line.reshape(8, cols, lanes)
        blur = taps_ref[0, v, 0] * lined[0:rows]
        for k in range(1, length):
            blur = blur + taps_ref[0, v, k] * lined[k : k + rows]
        spread[...] = obs[v] / blur
        for g in range(groups):
            pieces = []
            for e in range(8 * g, 8 * g + 8):
                piece = None
                for a in range(rows):
                    if 0 <= e - a < length:
                        term = taps_ref[0, v, e - a] * spread[a]
                        piece = term if piece is None else piece + term
                pieces.append(piece)
            piece = jnp.concatenate(pieces, axis=0)
            both = jnp.concatenate(split(piece), axis=1)
            piece = folded(dot(scat[v], jnp.concatenate([both, both], axis=0)))
            high, low = split(piece)
            flip = ((1,), (1,))
            piece = dot(jnp.concatenate([high, low], axis=1), twin[v], flip)
            piece = piece + dot(high, band[v, :, lanes:], flip)
            piece = piece.reshape(8, wide_y, 2 * lanes)
            dx = 0 if 8 * g < rad else (1 if 8 * g < rad + rows else 2)
            piece = piece * scale[v, dx][None]
            total[8 * g : 8 * g + 8] += piece[:, :, :lanes]
            fringe[8 * g : 8 * g + 8] += piece[:, :, lanes:]
        return carry

    lax.fori_loop(0, views, one_view, 0)

    for g in range(groups):
        merged = fringe[8 * g]
        for i in range(1, 8):
            merged = merged + pltpu.roll(fringe[8 * g + i], 2 * rad * i, 1)
        back_pack[g] = merged
    start(back_copies)
    arrive(back_copies)
    near = back_xy[...]

    def fold(values, size, rad, axis):
        low = lax.slice_in_dim(values, 0, rad, axis=axis)
        mid = lax.slice_in_dim(values, rad, rad + size, axis=axis)
        top = lax.slice_in_dim(values, rad + size, 2 * rad + size, axis=axis)
        if size == 2 * rad:
            return mid + jnp.concatenate([low, top], axis=axis)
        gap_shape = list(low.shape)
        gap_shape[axis] = size - rad
        gap = jnp.zeros(gap_shape, F32)
        return mid + jnp.concatenate([low, gap], axis=axis) + jnp.concatenate([gap, top], axis=axis)

    near = fold(fold(near, rows, rad, 0), cols, rad, 1)
    ends = jnp.where((lane % (2 * rad) < rad)[None], back_right[...], back_left[...])
    ends = fold(fold(ends, pack_rows, pack_rad, 0), cols, rad, 1)
    lane = lax.broadcasted_iota(jnp.int32, (cols, lanes), 1)
    outer = (lane < rad) | (lane >= lanes - rad)
    seen = jnp.zeros((8, lanes), F32)
    for x in range(rows):
        rolled = pltpu.roll(ends[x // 8], lanes - (2 * rad * (x % 8) + rad), 1)
        summed = total[rad + x, rad : rad + cols, :] + near[x] + jnp.where(outer, rolled, 0.0)
        updated = est_ref[x] * (summed / count)
        out_ref[x] = updated
        seen = seen + jnp.sum(updated.reshape(-1, 8, lanes), axis=0)
    stat[1:2] = jnp.sum(seen, axis=0, keepdims=True)

    def sums_a():
        for slot, offset in enumerate(ring_a):
            yield pltpu.make_async_remote_copy(
                src_ref=stat,
                dst_ref=stat_a.at[slot],
                send_sem=a_send.at[slot],
                recv_sem=a_recv.at[slot],
                device_id=partner(*offset),
                device_id_type=MESH,
            )

    def sums_b():
        for slot, offset in enumerate(ring_b):
            yield pltpu.make_async_remote_copy(
                src_ref=part_a,
                dst_ref=stat_b.at[slot],
                send_sem=b_send.at[slot],
                recv_sem=b_recv.at[slot],
                device_id=partner(*offset),
                device_id_type=MESH,
            )

    for copy in sums_a():
        copy.start()
    for copy in sums_a():
        copy.wait_recv()
    everything = stat[...] + jnp.sum(stat_a[...], axis=0)
    if ring_b:
        part_a[...] = everything
        for copy in sums_b():
            copy.start()
        for copy in sums_b():
            copy.wait_recv()
        everything = part_a[...] + jnp.sum(stat_b[...], axis=0)
    wanted = jnp.sum(everything[0:1], axis=1, keepdims=True)
    gotten = jnp.sum(everything[1:2], axis=1, keepdims=True)
    factor = jnp.broadcast_to(wanted, (1, lanes)) / jnp.broadcast_to(gotten, (1, lanes))
    out_ref[...] = out_ref[...] * factor.reshape(1, 1, lanes)

    for family in (out_copies, back_copies):
        leave(family)
    for copy in sums_a():
        copy.wait_send()
    for copy in sums_b():
        copy.wait_send()


def on_device(sizes, estimate, observed, coverage, psf_taps):
    rows, cols, lanes = estimate.shape
    views = observed.shape[0]
    rad = (psf_taps.shape[2] - 1) // 2
    wide_x, wide_y = rows + 2 * rad, cols + 2 * rad
    groups = wide_x // 8
    _, ring_a, ring_b = rings(sizes)
    n_a, n_b = len(ring_a), max(1, len(ring_b))

    def vm(*shape, dtype=F32):
        return pltpu.VMEM(shape, dtype)

    def dma(*shape):
        return pltpu.SemaphoreType.DMA(shape)

    scratch = [
        vm(*observed.shape),
        vm(wide_x, wide_y, lanes),
        vm(wide_x * wide_y, 2 * lanes, dtype=BF16),
        vm(wide_x * wide_y, 2 * lanes, dtype=BF16),
        vm(rows // 8, cols, lanes),
        vm(groups, wide_y, lanes),
        vm(groups, wide_y, lanes),
        vm(views, lanes),
        vm(3, 3, views, lanes),
        vm(3, 3, views, lanes),
        vm(3, 3, views, lanes),
        vm(views, 3, wide_y, 2 * lanes),
        vm(views, 2 * lanes, 2 * lanes, dtype=BF16),
        vm(views, 2 * lanes, 2 * lanes, dtype=BF16),
        vm(views, 8 * cols, 8 * wide_y, dtype=BF16),
        vm(views, 8 * cols, 8 * wide_y, dtype=BF16),
        vm(views, 8 * wide_y, 16 * cols, dtype=BF16),
        vm(wide_x, cols, lanes),
        vm(rows, cols, lanes),
        vm(wide_x, wide_y, lanes),
        vm(wide_x, wide_y, lanes),
        vm(groups, wide_y, lanes),
        vm(groups, wide_y, lanes),
        vm(groups, wide_y, lanes),
        vm(wide_x, wide_y, lanes),
        vm(2, lanes),
        vm(n_a, 2, lanes),
        vm(n_b, 2, lanes),
        vm(2, lanes),
        pltpu.SemaphoreType.DMA,
        dma(26, 2),
        dma(26, 2),
        dma(26),
        dma(26),
        dma(n_a),
        dma(n_a),
        dma(n_b),
        dma(n_b),
    ]
    return pl.pallas_call(
        functools.partial(kernel, sizes),
        out_shape=jax.ShapeDtypeStruct(estimate.shape, F32),
        in_specs=[
            pl.BlockSpec(memory_space=pltpu.SMEM),
            pl.BlockSpec(memory_space=pltpu.SMEM),
            pl.BlockSpec(memory_space=pltpu.VMEM),
            pl.BlockSpec(memory_space=pl.ANY),
        ],
        out_specs=pl.BlockSpec(memory_space=pltpu.VMEM),
        scratch_shapes=scratch,
        compiler_params=pltpu.CompilerParams(collective_id=0, has_side_effects=True),
    )(jnp.transpose(psf_taps, (1, 0, 2)), coverage.reshape(views), estimate, observed)


def solution(mesh):
    sizes = tuple(mesh.shape[axis] for axis in ("bx", "by", "bz"))
    return jax.shard_map(
        functools.partial(on_device, sizes),
        mesh=mesh,
        in_specs=(P("bx", "by", "bz"), P(None, "bx", "by", "bz"), P(None, "bx", "by", "bz"), P()),
        out_specs=P("bx", "by", "bz"),
        check_vma=False,
    )
```

time: 53.3 us -> 42 us (0.79)
  Pallas kernels: 50.1 us -> 40.2 us
  local copies, waits for them, and re-layouts: 2.88 us -> 1.57 us
    pallas_call x1, Pallas kernels: 50.1 us -> 40.2 us  [on_device(): pl.pallas_call(functools.partial(kernel, sizes), out_shape=jax.ShapeDtype...]
    unnamed x2 -> x1, local copies, waits for them, and re-layouts: 2.88 us -> 1.57 us
where the time goes in v1:
time: 42 us; the launch traced here: 41.8 us
  Pallas kernels  40.2 us (96%)
  local copies, waits for them, and re-layouts  1.57 us (4%)
    pallas_call x1, Pallas kernels, on_device(): pl.pallas_call(functools.partial(kernel, sizes), out_shape=jax.ShapeDtype...  40.2 us
    unnamed x1, local copies, waits for them, and re-layouts  1.57 us

profile of v1, /device:TPU:0, one launch (start us, length us, event | category | flops | bytes accessed | tf_op | source)
XLA Modules:
  0.0 41.8 jit_solution(8046402210755994608)
XLA Ops:
  0.0 40.2 %shard_map.46 = f32[16,16,128]{2,1,0:T(8,128)} custom-call(f32[3,8,17]{2,1,0:T(8,128)} %bitcast.2, s32[8]{0:T(128)} %bitcast.3, f32[16,16,128]{2,1,0:T(8,128)} %est_ref.1, f32[8,16,16,128]{3,2,1,0:T(8,128)} %obs_hbm.1), custom_call_target="tpu_custom_call" | custom-call | tf_op jit(solution)/shard_map/pallas_call | solution.py:483
  40.2 1.6 %copy.6 = f32[16,16,128]{2,1,0:T(8,128)} copy(f32[16,16,128]{2,1,0:T(8,128)} %shard_map.46) | data formatting | bytes 262144

commit v2 on v1

--- a/solution.py
+++ b/solution.py
@@ -342,7 +342,7 @@
             fringe[8 * g : 8 * g + 8] += piece[:, :, lanes:]
         return carry
 
-    lax.fori_loop(0, views, one_view, 0)
+    lax.fori_loop(0, views, one_view, 0, unroll=2)
 
     for g in range(groups):
         merged = fringe[8 * g]

time: 42 us -> 41.1 us (0.979)
  Pallas kernels: 40.2 us -> 39.3 us
    pallas_call x1, Pallas kernels: 40.2 us -> 39.3 us  [on_device(): pl.pallas_call(functools.partial(kernel, sizes), out_shape=jax.ShapeDtype...]
where the time goes in v2:
time: 41.1 us; the launch traced here: 40.9 us
  Pallas kernels  39.3 us (96%)
  local copies, waits for them, and re-layouts  1.57 us (4%)
    pallas_call x1, Pallas kernels, on_device(): pl.pallas_call(functools.partial(kernel, sizes), out_shape=jax.ShapeDtype...  39.3 us
    unnamed x1, local copies, waits for them, and re-layouts  1.57 us

profile of v2, /device:TPU:0, one launch (start us, length us, event | category | flops | bytes accessed | tf_op | source)
XLA Modules:
  0.0 40.9 jit_solution(7487917990581436118)
XLA Ops:
  0.0 39.3 %shard_map.46 = f32[16,16,128]{2,1,0:T(8,128)} custom-call(f32[3,8,17]{2,1,0:T(8,128)} %bitcast.2, s32[8]{0:T(128)} %bitcast.3, f32[16,16,128]{2,1,0:T(8,128)} %est_ref.1, f32[8,16,16,128]{3,2,1,0:T(8,128)} %obs_hbm.1), custom_call_target="tpu_custom_call" | custom-call | tf_op jit(solution)/shard_map/pallas_call | solution.py:483
  39.3 1.6 %copy.6 = f32[16,16,128]{2,1,0:T(8,128)} copy(f32[16,16,128]{2,1,0:T(8,128)} %shard_map.46) | data formatting | bytes 262144
